TPU v7x, 32 devices: a whole 2x2x4 slice. The times are simulated.
32 devices in a mesh: grp: 4 (over y, x), seq: 8 (over z, core).
Axes of the slice: x: 2, y: 2, z: 4, core: 2. Of those that a mesh axis runs over, the one named last changes fastest.
Arguments:
- queries: bfloat16 [8, 256, 8192], P('grp', 'seq'), parts along dimension 0, may hold values from -400 to 400
- stretch_keys: bfloat16 [8, 256, 1024], P('grp', 'seq'), parts along dimension 0, may hold values from -6 to 6
- stretch_values: bfloat16 [8, 256, 1024], P('grp', 'seq'), parts along dimension 0, may hold values from -6 to 6
- cache_keys: bfloat16 [8, 512, 1024], P('grp', 'seq'), parts along dimension 0, may hold values from -6 to 6
- cache_values: bfloat16 [8, 512, 1024], P('grp', 'seq'), parts along dimension 0, may hold values from -6 to 6
- prefix_len: int32 [8], P('grp'), parts along dimension 0, may hold values from 16 to 512, as said below
Outputs:
- attention: bfloat16 [8, 256, 8192], P('grp', 'seq'), parts along dimension 0
- prefix_bounds: bfloat16 [8, 32, 2048], P('grp', 'seq'), parts along dimension 0
- stretch_bounds: bfloat16 [8, 16, 2048], P('grp', 'seq'), parts along dimension 0
There are 4 independent parts, one for each index of `grp`. A program takes and returns all parts, laid end to end along the dimension named above; each array names one. Nothing has to cross between parts.
Inputs may be any that keep to these rules, and one draw needn't show every extreme that they name: `prefix_len`: multiples of 16; some sequence of every group has 512.
All inputs are finite; a program needn't handle non-finite values.
Results may differ from a plain program's by a relative error of at most 0.006.
Values may be sent and summed in bfloat16 or wider, within the bound.
A program may use at most 128 MiB of HBM per device.

v0:
```python
import math
import jax
import jax.numpy as jnp
from jax import lax
from jax.sharding import PartitionSpec as P

HQ = 64
HK = 8
DH = 128
PAGE = 16


def pick_block(length):
    for candidate in range(min(length, 512), 0, -1):
        if length % candidate == 0:
            return candidate
    return 1


def online(state, query_rows, query_pos, key_rows, value_rows, key_pos, from_cache, prefix_len):
    seqs, rows, _ = query_rows.shape
    group = HQ // HK
    factor = 1.0 / math.sqrt(DH)
    length = key_rows.shape[1]
    block = pick_block(length)
    steps_count = length // block
    shaped_query = query_rows.reshape(seqs, rows, HK, group, DH)
    key_blocks = jnp.moveaxis(key_rows.reshape(seqs, steps_count, block, HK, DH), 1, 0)
    value_blocks = jnp.moveaxis(value_rows.reshape(seqs, steps_count, block, HK, DH), 1, 0)
    pos_blocks = key_pos.reshape(steps_count, block)
    cache_blocks = from_cache.reshape(steps_count, block)
    top_length = jnp.max(prefix_len)
    top_query = jnp.max(query_pos)

    def one_step(current, pieces):
        key_part, value_part, pos_part, cache_part = pieces

        def compute(carried):
            running_top, running_sum, running_acc = carried
            scores = (
                jnp.einsum(
                    "srhgd,skhd->srhgk", shaped_query, key_part, preferred_element_type=jnp.float32
                )
                * factor
            )
            live = jnp.where(
                cache_part[None, None, :],
                pos_part[None, None, :] < prefix_len[:, None, None],
                pos_part[None, None, :] <= query_pos[None, :, None],
            )
            live = live[:, :, None, None, :]
            new_top = jnp.maximum(running_top, jnp.max(jnp.where(live, scores, -1e30), axis=-1))
            weights = jnp.where(live, jnp.exp(scores - new_top[..., None]), 0.0)
            shrink = jnp.exp(running_top - new_top)
            new_sum = running_sum * shrink + jnp.sum(weights, axis=-1)
            new_acc = running_acc * shrink[..., None] + jnp.einsum(
                "srhgk,skhd->srhgd",
                weights.astype(jnp.bfloat16),
                value_part,
                preferred_element_type=jnp.float32,
            )
            return (new_top, new_sum, new_acc)

        useful = jnp.any(jnp.where(cache_part, pos_part < top_length, pos_part <= top_query))
        return (lax.cond(useful, compute, lambda carried: carried, current), None)

    result, _ = lax.scan(one_step, state, (key_blocks, value_blocks, pos_blocks, cache_blocks))
    return result


def page_bounds(key_rows, live_pages):
    seqs, rows, width = key_rows.shape
    shaped = key_rows.reshape(seqs, rows // PAGE, PAGE, width)
    joined = jnp.concatenate([jnp.min(shaped, axis=2), jnp.max(shaped, axis=2)], axis=2)
    return jnp.where(live_pages[:, :, None], joined, jnp.zeros_like(joined))


def on_device(queries, stretch_keys, stretch_values, cache_keys, cache_values, prefix_len):
    seqs, ch_rows, _ = queries.shape
    pre_rows = cache_keys.shape[1]
    own_index = lax.axis_index("seq")
    group = HQ // HK
    groups = ((queries, own_index * ch_rows + jnp.arange(ch_rows, dtype=jnp.int32)),)
    states = tuple(
        (
            (
                jnp.full((seqs, entry[0].shape[1], HK, group), -1e30, jnp.float32),
                jnp.zeros((seqs, entry[0].shape[1], HK, group), jnp.float32),
                jnp.zeros((seqs, entry[0].shape[1], HK, group, DH), jnp.float32),
            )
            for entry in groups
        )
    )

    def absorb(current, key_rows, value_rows, key_pos, from_cache):
        return tuple(
            (
                online(
                    state, entry[0], entry[1], key_rows, value_rows, key_pos, from_cache, prefix_len
                )
                for state, entry in zip(current, groups)
            )
        )

    old_keys, old_values = (
        lax.all_gather(cache_keys, "seq", axis=1, tiled=True),
        lax.all_gather(cache_values, "seq", axis=1, tiled=True),
    )
    new_keys, new_values = (
        lax.all_gather(stretch_keys, "seq", axis=1, tiled=True),
        lax.all_gather(stretch_values, "seq", axis=1, tiled=True),
    )
    old_count = old_keys.shape[1]
    new_count = new_keys.shape[1]
    states = absorb(
        states,
        old_keys,
        old_values,
        jnp.arange(old_count, dtype=jnp.int32),
        jnp.ones((old_count,), bool),
    )
    states = absorb(
        states,
        new_keys,
        new_values,
        jnp.arange(new_count, dtype=jnp.int32),
        jnp.zeros((new_count,), bool),
    )
    outputs = [
        (state[2] / state[1][..., None])
        .reshape(seqs, state[2].shape[1], HQ * DH)
        .astype(jnp.bfloat16)
        for state in states
    ]
    attention = outputs[0]
    page_index = own_index * (pre_rows // PAGE) + jnp.arange(pre_rows // PAGE, dtype=jnp.int32)
    prefix_live = page_index[None, :] * PAGE < prefix_len[:, None]
    stretch_live = jnp.ones((seqs, ch_rows // PAGE), bool)
    return (
        attention,
        page_bounds(cache_keys, prefix_live),
        page_bounds(stretch_keys, stretch_live),
    )


def solution(mesh):
    return jax.shard_map(
        on_device,
        mesh=mesh,
        in_specs=(
            P("grp", "seq", None),
            P("grp", "seq", None),
            P("grp", "seq", None),
            P("grp", "seq", None),
            P("grp", "seq", None),
            P("grp"),
        ),
        out_specs=(P("grp", "seq", None), P("grp", "seq", None), P("grp", "seq", None)),
        check_vma=False,
    )
```

profile of v0, /device:TPU:0, one launch (start us, length us, event | category | flops | bytes accessed | tf_op | source)
XLA Modules:
  0.0 138.9 jit_solution(6246372038849168881)
XLA Ops:
  10.0 1.5 %copy.52 = bf16[8,8,64,128]{3,2,1,0:T(8,128)(2,1)S(1)} copy(bf16[8,8,64,128]{3,1,2,0:T(8,128)(2,1)} %bitcast.84) | data formatting | bytes 2097152
  12.2 1.3 fusion.28
  14.7 1.3 compare_reduce_fusion
  17.5 1.0 bitcast_reduce_fusion.3
  20.1 21.4 %all-gather.5.cloned.1.call-done = bf16[2,512,1024]{2,1,0:T(8,128)(2,1)} async-done(((bf16[2,64,1024]{2,1,0:T(8,128)(2,1)}), bf16[2,512,1024]{2,1,0:T(8,128)(2,1)}) %all-gather.5.cloned.1.call-update) | async-done | bytes 2097168 | tf_op jit(solution)/shard_map/all_gather | solution.py:106
  41.5 30.2 %all-gather.7.cloned.1.call-done = bf16[2,512,1024]{2,1,0:T(8,128)(2,1)} async-done(((bf16[2,64,1024]{2,1,0:T(8,128)(2,1)}), bf16[2,512,1024]{2,1,0:T(8,128)(2,1)}) %all-gather.7.cloned.1.call-update) | async-done | bytes 2097168 | tf_op jit(solution)/shard_map/all_gather | solution.py:107
  71.7 19.0 %conditional.2 = ((f32[2,32,8,8]{1,3,2,0:T(8,128)S(1)}, f32[2,32,8,8]{1,3,2,0:T(8,128)}, f32[2,32,8,8,128]{4,3,1,2,0:T(8,128)S(1)})) conditional(s32[]{:T(128)} %convert_element_type.24, (f32[2,32,8,8]{1,3,2,0:T(8,128)S(1)}, f32[2,32,8,8]{1,3,2,0:T(8,128)}, f32[2,32,8,8,128]{4,3,1,2,0:T(8,128)S(1)}) %tuple.36, (s32[512]{0:T(512)S(1)}, ...), branch_computations={%region_4.5_spmd, %region_5.8_spmd} | conditional | flops 1091576832 | bytes 68441152 | solution.py:65
  71.8 2.2 %copy.48 = bf16[128,8,8,128]{3,2,1,0:T(8,128)(2,1)S(1)} copy(bf16[128,8,8,128]{3,1,2,0:T(8,128)(2,1)} %bitcast.82) | data formatting | bytes 4194304 | tf_op jit(solution)/shard_map/while/body/eval_jaxpr/cond
  74.1 2.5 %fusion = (f32[2,32,8,8]{1,3,2,0:T(8,128)S(1)}, f32[2,8,512,32,8]{2,3,4,1,0:T(8,128)S(1)}) fusion(pred[2,512]{1,0:T(4,128)(4,1)S(1)} %broadcast_compare_fusion, bf16[2,32,8,8,128]{4,3,2,1,0:T(8,128)(2,1)S(1)} %get-tuple-element.213, bf16[2,512,8,128,1]{3,2,1,0,4:T(8,128)(2,1)S(1)} %bitcast_bitcast_fusion.1), kind=kOutput, calls=%fused_computation.2 | convolution fusion | flops 543158272 | bytes 11551744 | tf_op jit(solution)/shard_map/while/body/eval_jaxpr/cond/branch_1_fun/srhgd,skhd->srhgk/dot_general | solution.py:41
  76.6 3.6 %fusion.3 = (bf16[2,32,8,8,512]{4,1,3,2,0:T(8,128)(2,1)}, f32[2,32,8,8]{1,3,2,0:T(8,128)S(1)}) fusion(f32[2,8,512,32,8]{2,3,4,1,0:T(8,128)S(1)} %get-tuple-element.255, f32[2,32,8,8]{1,3,2,0:T(8,128)S(1)} %max.7, pred[2,512]{1,0:T(4,128)(4,1)S(1)} %broadcast_compare_fusion), kind=kLoop, calls=%fused_computation.5 | loop fusion | flops 10481664 | bytes 12616704 | tf_op jit(solution)/shard_map/while/body/eval_jaxpr/cond/branch_1_fun/convert_element_type | solution.py:58
  80.2 1.5 %multiply_add_fusion = (f32[2,32,8,8]{1,3,2,0:T(8,128)}, f32[2,32,8,8]{1,3,2,0:T(8,128)}) fusion(f32[2,32,8,8]{1,3,2,0:T(8,128)S(1)} %get-tuple-element.253, f32[2,32,8,8]{1,3,2,0:T(8,128)} %get-tuple-element.184, f32[2,32,8,8]{1,3,2,0:T(8,128)S(1)} %get-tuple-element.179, f32[2,32,8,8]{1,3,2,0:T(8,128)S(1)} %max.7), kind=kLoop, calls=%fused_computation.16 | loop fusion | flops 12288 | bytes 98304 | tf_op jit(solution)/shard_map/while/body/eval_jaxpr/cond/branch_1_fun/add | solution.py:55
  82.7 2.2 %copy.49 = bf16[128,8,8,128]{3,2,1,0:T(8,128)(2,1)S(1)} copy(bf16[128,8,8,128]{3,1,2,0:T(8,128)(2,1)} %bitcast.83) | data formatting | bytes 4194304 | tf_op jit(solution)/shard_map/while/body/eval_jaxpr/cond
  85.1 2.1 %copy-done.1 = bf16[2,32,8,8,512]{4,1,3,2,0:T(8,128)(2,1)S(1)} copy-done((bf16[2,32,8,8,512]{4,1,3,2,0:T(8,128)(2,1)S(1)}, bf16[2,32,8,8,512]{4,1,3,2,0:T(8,128)(2,1)}, u32[]{:S(2)}) %copy-start.1) | copy-done | bytes 4194328 | tf_op jit(solution)/shard_map/while/body/eval_jaxpr/cond
  87.2 3.4 %bitcast_add_fusion = f32[2,32,8,8,128]{4,3,1,2,0:T(8,128)S(1)} fusion(f32[2,32,8,8,128]{4,3,1,2,0:T(8,128)S(1)} %get-tuple-element.185, bf16[2,512,8,128,1]{3,2,1,0,4:T(8,128)(2,1)S(1)} %bitcast_bitcast_fusion, bf16[2,32,8,8,512]{4,1,3,2,0:T(8,128)(2,1)S(1)} %copy-done.1, f32[2,32,8,8]{3,1,2,0:T(8,128)S(1)} %copy.20), kind=kOutput, calls=%fused_computation.11 | convolution fusion | flops 537919488 | bytes 10502144 | tf_op jit(solution)/shard_map/while/body/eval_jaxpr/cond/branch_1_fun/srhgk,skhd->srhgd/dot_general | solution.py:56
  90.7 4.3 %all-gather.11.cloned.1.call-done = bf16[2,256,1024]{2,1,0:T(8,128)(2,1)} async-done(((bf16[2,32,1024]{2,1,0:T(8,128)(2,1)}), bf16[2,256,1024]{2,1,0:T(8,128)(2,1)}) %all-gather.11.cloned.1.call-update) | async-done | bytes 1048592 | tf_op jit(solution)/shard_map/all_gather | solution.py:111
  95.0 23.3 %all-gather.9.cloned.1.call-done = bf16[2,256,1024]{2,1,0:T(8,128)(2,1)} async-done(((bf16[2,32,1024]{2,1,0:T(8,128)(2,1)}), bf16[2,256,1024]{2,1,0:T(8,128)(2,1)}) %all-gather.9.cloned.1.call-update) | async-done | bytes 1048592 | tf_op jit(solution)/shard_map/all_gather | solution.py:110
  118.3 10.8 %conditional.3 = ((f32[2,32,8,8]{1,3,2,0:T(8,128)}, f32[2,32,8,8,128]{4,3,1,2,0:T(8,128)S(1)})) conditional(s32[]{:T(128)} %convert_element_type.23, (f32[2,32,8,8]{1,3,2,0:T(8,128)}, f32[2,32,8,8,128]{4,3,1,2,0:T(8,128)S(1)}) %tuple.38, (s32[256]{0:T(256)S(1)}, s32[32]{0:T(128)S(1)}, bf16[2,256,1024]{2,1,0:T(8,128)(2,1)}, ...), branch_computations={%region_8.9_spmd, %region_9.12_spmd.clone} | conditional | flops 546324480 | bytes 41166032 | solution.py:65
  118.4 1.5 %copy.50 = bf16[64,8,8,128]{3,2,1,0:T(8,128)(2,1)S(1)} copy(bf16[64,8,8,128]{3,1,2,0:T(8,128)(2,1)} %bitcast.86) | data formatting | bytes 2097152 | tf_op jit(solution)/shard_map/while/body/eval_jaxpr/cond
  119.9 1.4 fusion.15
  121.3 2.5 %fusion.18 = (bf16[2,32,8,8,256]{4,1,3,2,0:T(8,128)(2,1)}, f32[2,32,8,8]{1,3,2,0:T(8,128)S(1)}) fusion(f32[2,8,256,32,8]{2,3,4,1,0:T(8,128)S(1)} %get-tuple-element.259, f32[2,32,8,8]{1,3,2,0:T(8,128)S(1)} %max.9, pred[32,256]{1,0:T(8,128)(4,1)S(1)} %broadcast_compare_fusion.1), kind=kLoop, calls=%fused_computation.24 | loop fusion | flops 5238784 | bytes 6332416 | tf_op jit(solution)/shard_map/while/body/eval_jaxpr/cond/branch_1_fun/convert_element_type | solution.py:58
  123.8 1.5 %multiply_add_fusion.1 = (f32[2,32,8,8]{1,3,2,0:T(8,128)}, f32[2,32,8,8]{1,3,2,0:T(8,128)S(1)}) fusion(f32[2,32,8,8]{1,3,2,0:T(8,128)S(1)} %get-tuple-element.257, f32[2,32,8,8]{1,3,2,0:T(8,128)} %get-tuple-element.233, f32[2,32,8,8]{1,3,2,0:T(8,128)S(1)} %get-tuple-element.232, f32[2,32,8,8]{1,3,2,0:T(8,128)S(1)} %max.9), kind=kLoop, calls=%fused_computation.35 | loop fusion | flops 12288 | bytes 98304 | tf_op jit(solution)/shard_map/while/body/eval_jaxpr/cond/branch_1_fun/add | solution.py:55
  125.8 1.2 copy-done
  127.0 2.0 %bitcast_add_fusion.1 = f32[2,32,8,8,128]{4,3,1,2,0:T(8,128)S(1)} fusion(f32[2,32,8,8,128]{4,3,1,2,0:T(8,128)S(1)} %get-tuple-element.234, bf16[2,32,8,8,256]{4,1,3,2,0:T(8,128)(2,1)S(1)} %copy-done, bf16[2,256,8,128,1]{3,2,1,0,4:T(8,128)(2,1)S(1)} %bitcast_bitcast_fusion.2, f32[2,32,8,8]{3,1,2,0:T(8,128)S(1)} %copy.43), kind=kOutput, calls=%fused_computation.26 | convolution fusion | flops 269484032 | bytes 7356416 | tf_op jit(solution)/shard_map/while/body/eval_jaxpr/cond/branch_1_fun/srhgk,skhd->srhgd/dot_general | solution.py:56
  131.1 1.3 convert_element_type.26
  (44 shorter events, 10.3 us)
Async XLA Ops:
  7.2 4.4 %copy-start.4 = (s32[2]{0:T(128)S(1)}, s32[2]{0:T(128)}, u32[]{:S(2)}) copy-start(s32[2]{0:T(128)} %param.15) | copy-start | bytes 28
  7.2 34.3 %all-gather.5.cloned.1.call-start = ((), (), s32[]{:S(2)}) async-start(), calls=%async_computation | async-start | bytes 2359296 | tf_op jit(solution)/shard_map/all_gather | solution.py:106
  7.9 63.8 %all-gather.7.cloned.1.call-start = ((), (), s32[]{:S(2)}) async-start(), calls=%async_computation.1 | async-start | bytes 2359296 | tf_op jit(solution)/shard_map/all_gather | solution.py:107
  8.7 86.3 %all-gather.11.cloned.1.call-start = ((), (), s32[]{:S(2)}) async-start(), calls=%async_computation.3 | async-start | bytes 1179648 | tf_op jit(solution)/shard_map/all_gather | solution.py:111
  9.4 108.9 %all-gather.9.cloned.1.call-start = ((), (), s32[]{:S(2)}) async-start(), calls=%async_computation.2 | async-start | bytes 1179648 | tf_op jit(solution)/shard_map/all_gather | solution.py:110
  10.0 8.6 %copy-start.3 = (bf16[2,64,1024]{2,1,0:T(8,128)(2,1)S(1)}, bf16[2,64,1024]{2,1,0:T(8,128)(2,1)}, u32[]{:S(2)}) copy-start(bf16[2,64,1024]{2,1,0:T(8,128)(2,1)} %param.13) | copy-start | bytes 786436
  84.9 2.3 %copy-start.1 = (bf16[2,32,8,8,512]{4,1,3,2,0:T(8,128)(2,1)S(1)}, bf16[2,32,8,8,512]{4,1,3,2,0:T(8,128)(2,1)}, u32[]{:S(2)}) copy-start(bf16[2,32,8,8,512]{4,1,3,2,0:T(8,128)(2,1)} %get-tuple-element.252) | copy-start | bytes 12582916 | tf_op jit(solution)/shard_map/while/body/eval_jaxpr/cond
  121.3 4.1 %copy-start.2 = (bf16[2,256,1024]{2,1,0:T(8,128)(2,1)S(1)}, bf16[2,256,1024]{2,1,0:T(8,128)(2,1)}, u32[]{:S(2)}) copy-start(bf16[2,256,1024]{2,1,0:T(8,128)(2,1)} %get-tuple-element.235) | copy-start | bytes 3145732 | tf_op jit(solution)/shard_map/while/body/eval_jaxpr/cond
  125.4 1.6 %copy-start = (bf16[2,32,8,8,256]{4,1,3,2,0:T(8,128)(2,1)S(1)}, bf16[2,32,8,8,256]{4,1,3,2,0:T(8,128)(2,1)}, u32[]{:S(2)}) copy-start(bf16[2,32,8,8,256]{4,1,3,2,0:T(8,128)(2,1)} %get-tuple-element.256) | copy-start | bytes 6291460 | tf_op jit(solution)/shard_map/while/body/eval_jaxpr/cond
Sparse Core Ops, SparseCore 0:
  9.6 31.8 all-gather.4
  43.1 28.5 all-gather.6
  73.3 21.6 all-gather.10
  96.4 21.8 all-gather.8
where the time goes:
time: 139 us
  waiting for transfers between devices  81.8 us (59%)
  other arithmetic  16.4 us (12%)
  local copies, waits for them, and re-layouts  15.9 us (11%)
  between operations  15.2 us (11%)
  matrix products  9.3 us (7%)
    all_gather x1, waiting for transfers between devices, on_device(): lax.all_gather(cache_values, 'seq', axis=1, tiled=True)  30.2 us
    all_gather x1, waiting for transfers between devices, on_device(): lax.all_gather(stretch_keys, 'seq', axis=1, tiled=True)  23.3 us
    all_gather x1, waiting for transfers between devices, on_device(): lax.all_gather(cache_keys, 'seq', axis=1, tiled=True)  21.4 us
    cond x11, local copies, waits for them, and re-layouts  9.53 us
    convert_element_type x2, other arithmetic, compute(): weights.astype(jnp.bfloat16)  6.11 us
    dot_general x2, matrix products, compute(): jnp.einsum('srhgk,skhd->srhgd', weights.astype(jnp.bfloat16), value_part,...  5.48 us
    all_gather x1, waiting for transfers between devices, on_device(): lax.all_gather(stretch_values, 'seq', axis=1, tiled=True)  4.29 us
    dot_general x2, matrix products, compute(): jnp.einsum('srhgd,skhd->srhgk', shaped_query, key_part, preferred_element...  3.81 us
  transfers between devices with their start and end apart: 4, of which 4 were waited for; matrix products, arithmetic and copies ran while one was open for 18% of the time, Pallas kernels for 0%

commit v1 on v0

--- a/solution.py
+++ b/solution.py
@@ -107,7 +107,9 @@
         lax.all_gather(cache_values, "seq", axis=1, tiled=True),
     )
     new_keys, new_values = (
-        lax.all_gather(stretch_keys, "seq", axis=1, tiled=True),
+        jnp.concatenate(
+            lax.all_to_all(jnp.stack([stretch_keys] * lax.axis_size("seq")), "seq", 0, 0), axis=1
+        ),
         lax.all_gather(stretch_values, "seq", axis=1, tiled=True),
     )
     old_count = old_keys.shape[1]

time: 139 us -> 132 us (0.950)
  waiting for transfers between devices: 81.8 us -> 69.3 us
  starting transfers between devices: 0.15 us -> 6.6 us
  other arithmetic: 16.4 us -> 13.4 us
    all_gather x1 -> x0, waiting for transfers between devices: 23.3 us -> none  [on_device(): lax.all_gather(stretch_keys, 'seq', axis=1, tiled=True)]
    all_gather x1, waiting for transfers between devices: 21.4 us -> 33.5 us  [on_device(): lax.all_gather(cache_keys, 'seq', axis=1, tiled=True)]
    all_to_all x0 -> x1, starting transfers between devices: none -> 6.49 us  [on_device(): lax.all_to_all(jnp.stack([stretch_keys] * lax.axis_size('seq')), 'seq', 0...]
    add x2, other arithmetic: 3 us -> 0.08 us  [compute(): new_sum = running_sum * shrink + jnp.sum(weights, axis=-1)]
    another operation x0 -> x2, local copies, waits for them, and re-layouts: none -> 2.1 us  [the longest x1 2.01 us: on_device(): jnp.stack([stretch_keys] * lax.axis_size('seq'))]
    cond x11 -> x15, local copies, waits for them, and re-layouts: 9.53 us -> 10.6 us
  transfers between devices with their start and end apart: 4 -> 4, of which waited for: 4 -> 3; matrix products, arithmetic and copies ran while one was open for 18% -> 19% of each run, Pallas kernels for 0% -> 0%
where the time goes in v1:
time: 132 us; the launch traced here: 131 us
  waiting for transfers between devices  69.3 us (52%)
  local copies, waits for them, and re-layouts  17.2 us (13%)
  between operations  15.2 us (12%)
  other arithmetic  13.4 us (10%)
  matrix products  9.32 us (7%)
  starting transfers between devices  6.6 us (5%)
    all_gather x1, waiting for transfers between devices, on_device(): lax.all_gather(cache_keys, 'seq', axis=1, tiled=True)  33.5 us
    all_gather x1, waiting for transfers between devices, on_device(): lax.all_gather(cache_values, 'seq', axis=1, tiled=True)  29 us
    cond x15, local copies, waits for them, and re-layouts  10.6 us
    all_to_all x1, starting transfers between devices, on_device(): lax.all_to_all(jnp.stack([stretch_keys] * lax.axis_size('seq')), 'seq', 0...  6.49 us
    convert_element_type x2, other arithmetic, compute(): weights.astype(jnp.bfloat16)  6.11 us
    dot_general x2, matrix products, compute(): jnp.einsum('srhgk,skhd->srhgd', weights.astype(jnp.bfloat16), value_part,...  5.49 us
    all_gather x1, waiting for transfers between devices, on_device(): lax.all_gather(stretch_values, 'seq', axis=1, tiled=True)  4.76 us
    dot_general x2, matrix products, compute(): jnp.einsum('srhgd,skhd->srhgk', shaped_query, key_part, preferred_element...  3.83 us
  transfers between devices with their start and end apart: 4, of which 3 were waited for; matrix products, arithmetic and copies ran while one was open for 19% of the time, Pallas kernels for 0%

profile of v1, /device:TPU:0, one launch (start us, length us, event | category | flops | bytes accessed | tf_op | source)
XLA Modules:
  0.0 131.2 jit_solution(1159934436430674868)
XLA Ops:
  8.7 2.0 %stack.2 = bf16[8,2,32,1024]{3,2,1,0:T(8,128)(2,1)} broadcast(bf16[2,32,1024]{2,1,0:T(8,128)(2,1)} %param.11), dimensions={1,2,3} | broadcast | bytes 1179648 | tf_op jit(solution)/shard_map/stack | solution.py:111
  10.7 6.5 %all-to-all-start = ((bf16[8,2,32,1024]{3,2,1,0:T(8,128)(2,1)}), bf16[8,2,32,1024]{3,2,1,0:T(8,128)(2,1)S(1)}, u32[]{:S(2)}, u32[]{:S(2)}) async-start(bf16[8,2,32,1024]{3,2,1,0:T(8,128)(2,1)} %stack.2), calls=%async_computation | async-start | bytes 2097152 | tf_op jit(solution)/shard_map/all_to_all | solution.py:111
  17.9 1.3 copy.66
  19.8 1.3 fusion.28
  22.4 1.3 compare_reduce_fusion
  24.6 1.0 bitcast_reduce_fusion.3
  27.1 33.5 %all-gather.4.cloned.1.call-done = bf16[2,512,1024]{2,1,0:T(8,128)(2,1)} async-done(((bf16[2,64,1024]{2,1,0:T(8,128)(2,1)}), bf16[2,512,1024]{2,1,0:T(8,128)(2,1)}) %all-gather.4.cloned.1.call-update) | async-done | bytes 2097168 | tf_op jit(solution)/shard_map/all_gather | solution.py:106
  60.6 29.0 %all-gather.6.cloned.1.call-done = bf16[2,512,1024]{2,1,0:T(8,128)(2,1)} async-done(((bf16[2,64,1024]{2,1,0:T(8,128)(2,1)}), bf16[2,512,1024]{2,1,0:T(8,128)(2,1)}) %all-gather.6.cloned.1.call-update) | async-done | bytes 2097168 | tf_op jit(solution)/shard_map/all_gather | solution.py:107
  89.6 18.5 %conditional.2 = ((f32[2,32,8,8]{1,3,2,0:T(8,128)S(1)}, f32[2,32,8,8]{1,3,2,0:T(8,128)S(1)}, f32[2,32,8,8,128]{4,3,1,2,0:T(8,128)S(1)})) conditional(s32[]{:T(128)} %convert_element_type.24, (f32[2,32,8,8]{1,3,2,0:T(8,128)S(1)}, f32[2,32,8,8]{1,3,2,0:T(8,128)S(1)}, f32[2,32,8,8,128]{4,3,1,2,0:T(8,128)S(1)}) %tuple.36, (s32[512]{0:T(512)S(1)}, ...), branch_computations={%region_4.5_spmd, %region_5.8_spmd} | conditional | flops 1091576832 | bytes 72701056 | solution.py:65
  89.6 2.2 %copy.62 = bf16[128,8,8,128]{3,2,1,0:T(8,128)(2,1)S(1)} copy(bf16[128,8,8,128]{3,1,2,0:T(8,128)(2,1)} %bitcast.86) | data formatting | bytes 4194304 | tf_op jit(solution)/shard_map/while/body/eval_jaxpr/cond
  92.0 1.1 copy-done.3
  93.1 2.5 %fusion = (f32[2,32,8,8]{1,3,2,0:T(8,128)S(1)}, f32[2,8,512,32,8]{2,3,4,1,0:T(8,128)S(1)}) fusion(pred[2,512]{1,0:T(4,128)(4,1)S(1)} %broadcast_compare_fusion, bf16[2,32,8,8,128]{4,3,2,1,0:T(8,128)(2,1)S(1)} %copy-done.3, bf16[2,512,8,128,1]{3,2,1,0,4:T(8,128)(2,1)S(1)} %bitcast_bitcast_fusion.1), kind=kOutput, calls=%fused_computation.2 | convolution fusion | flops 543158272 | bytes 11551744 | tf_op jit(solution)/shard_map/while/body/eval_jaxpr/cond/branch_1_fun/srhgd,skhd->srhgk/dot_general | solution.py:41
  95.6 3.6 %fusion.3 = (bf16[2,32,8,8,512]{4,1,3,2,0:T(8,128)(2,1)}, f32[2,32,8,8]{1,3,2,0:T(8,128)S(1)}) fusion(f32[2,8,512,32,8]{2,3,4,1,0:T(8,128)S(1)} %get-tuple-element.273, f32[2,32,8,8]{1,3,2,0:T(8,128)S(1)} %max.7, pred[2,512]{1,0:T(4,128)(4,1)S(1)} %broadcast_compare_fusion), kind=kLoop, calls=%fused_computation.5 | loop fusion | flops 10481664 | bytes 12616704 | tf_op jit(solution)/shard_map/while/body/eval_jaxpr/cond/branch_1_fun/convert_element_type | solution.py:58
  100.1 2.3 %copy.63 = bf16[128,8,8,128]{3,2,1,0:T(8,128)(2,1)S(1)} copy(bf16[128,8,8,128]{3,1,2,0:T(8,128)(2,1)} %bitcast.87) | data formatting | bytes 4194304 | tf_op jit(solution)/shard_map/while/body/eval_jaxpr/cond
  102.5 2.1 %copy-done.1 = bf16[2,32,8,8,512]{4,1,3,2,0:T(8,128)(2,1)S(1)} copy-done((bf16[2,32,8,8,512]{4,1,3,2,0:T(8,128)(2,1)S(1)}, bf16[2,32,8,8,512]{4,1,3,2,0:T(8,128)(2,1)}, u32[]{:S(2)}) %copy-start.1) | copy-done | bytes 4194328 | tf_op jit(solution)/shard_map/while/body/eval_jaxpr/cond
  104.6 3.5 %bitcast_add_fusion = f32[2,32,8,8,128]{4,3,1,2,0:T(8,128)S(1)} fusion(f32[2,32,8,8,128]{4,3,1,2,0:T(8,128)S(1)} %get-tuple-element.185, bf16[2,512,8,128,1]{3,2,1,0,4:T(8,128)(2,1)S(1)} %bitcast_bitcast_fusion, bf16[2,32,8,8,512]{4,1,3,2,0:T(8,128)(2,1)S(1)} %copy-done.1, f32[2,32,8,8]{3,1,2,0:T(8,128)S(1)} %copy-done.6), kind=kOutput, calls=%fused_computation.11 | convolution fusion | flops 537919488 | bytes 10502144 | tf_op jit(solution)/shard_map/while/body/eval_jaxpr/cond/branch_1_fun/srhgk,skhd->srhgd/dot_general | solution.py:56
  108.1 4.8 %all-gather.8.cloned.1.call-done = bf16[2,256,1024]{2,1,0:T(8,128)(2,1)} async-done(((bf16[2,32,1024]{2,1,0:T(8,128)(2,1)}), bf16[2,256,1024]{2,1,0:T(8,128)(2,1)}) %all-gather.8.cloned.1.call-update) | async-done | bytes 1048592 | tf_op jit(solution)/shard_map/all_gather | solution.py:113
  112.8 9.4 %conditional.3 = ((f32[2,32,8,8]{1,3,2,0:T(8,128)S(1)}, f32[2,32,8,8,128]{4,3,1,2,0:T(8,128)S(1)})) conditional(s32[]{:T(128)} %convert_element_type.23, (f32[2,32,8,8]{1,3,2,0:T(8,128)S(1)}, f32[2,32,8,8,128]{4,3,1,2,0:T(8,128)S(1)}) %tuple.38, (s32[256]{0:T(256)S(1)}, s32[32]{0:T(128)S(1)}, bf16[2,8,32,1024]{3,2,0,1:T(8,128)(2,1)S(1)}, ...), branch_computations={%region_8.9_spmd, %region_9.12_spmd.clone} | conditional | flops 546324480 | bytes 43263184 | solution.py:65
  113.4 0.9 copy-done.4
  114.3 1.3 %fusion.15 = (f32[2,32,8,8]{1,3,2,0:T(8,128)S(1)}, f32[2,8,256,32,8]{2,3,4,1,0:T(8,128)S(1)}) fusion(pred[32,256]{1,0:T(8,128)(4,1)S(1)} %broadcast_compare_fusion.1, bf16[2,32,8,8,128]{4,3,2,1,0:T(8,128)(2,1)S(1)} %copy-done.4, bf16[2,256,8,128,1]{3,2,1,0,4:T(8,128)(2,1)S(1)} %bitcast_bitcast_fusion.3), kind=kOutput, calls=%fused_computation.21 | convolution fusion | flops 271577088 | bytes 6316032 | tf_op jit(solution)/shard_map/while/body/eval_jaxpr/cond/branch_1_fun/srhgd,skhd->srhgk/dot_general | solution.py:41
  115.6 2.5 %fusion.18 = (bf16[2,32,8,8,256]{4,1,3,2,0:T(8,128)(2,1)}, f32[2,32,8,8]{1,3,2,0:T(8,128)S(1)}) fusion(f32[2,8,256,32,8]{2,3,4,1,0:T(8,128)S(1)} %get-tuple-element.277, f32[2,32,8,8]{1,3,2,0:T(8,128)S(1)} %max.9, pred[32,256]{1,0:T(8,128)(4,1)S(1)} %broadcast_compare_fusion.1), kind=kLoop, calls=%fused_computation.24 | loop fusion | flops 5238784 | bytes 6332416 | tf_op jit(solution)/shard_map/while/body/eval_jaxpr/cond/branch_1_fun/convert_element_type | solution.py:58
  118.3 1.6 %copy.65 = bf16[64,8,8,128]{3,2,1,0:T(8,128)(2,1)S(1)} copy(bf16[64,8,8,128]{3,1,2,0:T(8,128)(2,1)} %bitcast.89) | data formatting | bytes 2097152 | tf_op jit(solution)/shard_map/while/body/eval_jaxpr/cond
  120.2 2.0 %bitcast_add_fusion.1 = f32[2,32,8,8,128]{4,3,1,2,0:T(8,128)S(1)} fusion(f32[2,32,8,8,128]{4,3,1,2,0:T(8,128)S(1)} %get-tuple-element.252, bf16[2,32,8,8,256]{4,1,3,2,0:T(8,128)(2,1)S(1)} %copy-done, bf16[2,256,8,128,1]{3,2,1,0,4:T(8,128)(2,1)S(1)} %bitcast_bitcast_fusion.2, f32[2,32,8,8]{3,1,2,0:T(8,128)S(1)} %copy.56), kind=kOutput, calls=%fused_computation.26 | convolution fusion | flops 269484032 | bytes 7356416 | tf_op jit(solution)/shard_map/while/body/eval_jaxpr/cond/branch_1_fun/srhgk,skhd->srhgd/dot_general | solution.py:56
  123.4 1.3 convert_element_type.26
  (51 shorter events, 8.5 us)
Async XLA Ops:
  7.2 10.7 %copy-start.2 = (bf16[2,32,8192]{2,1,0:T(8,128)(2,1)S(1)}, bf16[2,32,8192]{2,1,0:T(8,128)(2,1)}, u32[]{:S(2)}) copy-start(bf16[2,32,8192]{2,1,0:T(8,128)(2,1)} %param.10) | copy-start | bytes 3145732
  7.2 53.4 %all-gather.4.cloned.1.call-start = ((), (), s32[]{:S(2)}) async-start(), calls=%async_computation.1 | async-start | bytes 2359296 | tf_op jit(solution)/shard_map/all_gather | solution.py:106
  7.9 81.7 %all-gather.6.cloned.1.call-start = ((), (), s32[]{:S(2)}) async-start(), calls=%async_computation.2 | async-start | bytes 2359296 | tf_op jit(solution)/shard_map/all_gather | solution.py:107
  10.7 8.5 %copy-start.7 = (s32[2]{0:T(128)S(1)}, s32[2]{0:T(128)}, u32[]{:S(2)}) copy-start(s32[2]{0:T(128)} %param.15) | copy-start | bytes 28
  10.7 97.4 %all-to-all-start = ((bf16[8,2,32,1024]{3,2,1,0:T(8,128)(2,1)}), bf16[8,2,32,1024]{3,2,1,0:T(8,128)(2,1)S(1)}, u32[]{:S(2)}, u32[]{:S(2)}) async-start(bf16[8,2,32,1024]{3,2,1,0:T(8,128)(2,1)} %stack.2), calls=%async_computation | async-start | bytes 2097152 | tf_op jit(solution)/shard_map/all_to_all | solution.py:111
  17.2 95.7 %all-gather.8.cloned.1.call-start = ((), (), s32[]{:S(2)}) async-start(), calls=%async_computation.3 | async-start | bytes 1179648 | tf_op jit(solution)/shard_map/all_gather | solution.py:113
  17.9 7.7 %copy-start.5 = (bf16[2,64,1024]{2,1,0:T(8,128)(2,1)S(1)}, bf16[2,64,1024]{2,1,0:T(8,128)(2,1)}, u32[]{:S(2)}) copy-start(bf16[2,64,1024]{2,1,0:T(8,128)(2,1)} %param.13) | copy-start | bytes 786436
  91.9 1.2 copy-start.3
  100.1 2.4 %copy-start.6 = (f32[2,32,8,8]{3,1,2,0:T(8,128)S(1)}, f32[2,32,8,8]{3,1,2,0:T(8,128)}, u32[]{:S(2)}) copy-start(f32[2,32,8,8]{3,1,2,0:T(8,128)} %copy.32) | copy-start | bytes 49156 | tf_op jit(solution)/shard_map/while/body/eval_jaxpr/cond
  102.4 2.2 %copy-start.1 = (bf16[2,32,8,8,512]{4,1,3,2,0:T(8,128)(2,1)S(1)}, bf16[2,32,8,8,512]{4,1,3,2,0:T(8,128)(2,1)}, u32[]{:S(2)}) copy-start(bf16[2,32,8,8,512]{4,1,3,2,0:T(8,128)(2,1)} %get-tuple-element.270) | copy-start | bytes 12582916 | tf_op jit(solution)/shard_map/while/body/eval_jaxpr/cond
  113.0 1.2 copy-start.4
  118.3 1.9 %copy-start = (bf16[2,32,8,8,256]{4,1,3,2,0:T(8,128)(2,1)S(1)}, bf16[2,32,8,8,256]{4,1,3,2,0:T(8,128)(2,1)}, u32[]{:S(2)}) copy-start(bf16[2,32,8,8,256]{4,1,3,2,0:T(8,128)(2,1)} %get-tuple-element.274) | copy-start | bytes 6291460 | tf_op jit(solution)/shard_map/while/body/eval_jaxpr/cond
Sparse Core Ops, SparseCore 0:
  9.6 50.9 all-gather.3
  62.2 27.3 all-gather.5
  91.2 21.6 all-gather.7
